TPU v7x, 32 devices: a whole 2x2x4 slice. The times are simulated.
32 devices in a mesh: dom: 8 (over z, x), sub: 4 (over y, core).
Axes of the slice: x: 2, y: 2, z: 4, core: 2. Of those that a mesh axis runs over, the one named last changes fastest.
Arguments:
- level_set: float32 [64, 32, 128], P('dom', 'sub'), may hold values from 0 to 1
- velocity: float32 [3, 64, 32, 128], P(None, 'dom', 'sub'), may hold values from -6 to 6
- source: float32 [64, 32, 128], P('dom', 'sub'), may hold values from -12 to 12
Outputs:
- new_level: float32 [64, 32, 128], P('dom', 'sub')
- pressure: float32 [64, 32, 128], P('dom', 'sub')
- correction: float32 [64, 32, 128], P('dom', 'sub')
All inputs are finite; a program needn't handle non-finite values.
Results may differ from a plain program's by a relative error of at most 0.0003.
Values sent between devices are 32-bit elements; how exact they have to be, the bound alone decides.
A program may use at most 64 MiB of HBM per device.

v0:
```python
import math
import jax
import jax.numpy as jnp
import numpy as np
from jax import lax
from jax.sharding import PartitionSpec as P

SWEEPS = 2
PITERS = 2
gll_nodes = [
    -1.0,
    -0.8717401485096066,
    -0.5917001814331423,
    -0.2092992179024789,
    0.2092992179024789,
    0.5917001814331423,
    0.8717401485096066,
    1.0,
]
advect_step = 0.05
reinit_step = 0.02
interface_width = 0.1
density_ratio = 9.0


def padded(x, sides, width):
    for axis, dim in sides:
        devices, length = (lax.axis_size(axis), x.shape[dim])
        up = [(i, (i + 1) % devices) for i in range(devices)]
        down = [(j, i) for i, j in up]
        last = lax.slice_in_dim(x, length - width, length, axis=dim)
        leading = lax.slice_in_dim(x, 0, width, axis=dim)
        before = lax.ppermute(last, axis, up)
        after = lax.ppermute(leading, axis, down)
        x = jnp.concatenate([before, x, after], axis=dim)
    return x


def tables():
    node_points = np.array(gll_nodes)
    poly_order = 7
    values_prev = np.ones(8)
    values_now = node_points.copy()
    for degree in range(1, poly_order):
        values_next = ((2 * degree + 1) * node_points * values_now - degree * values_prev) / (
            degree + 1
        )
        values_prev, values_now = (values_now, values_next)
    matrix = np.zeros((8, 8))
    for line in range(8):
        for column in range(8):
            if line != column:
                matrix[line, column] = values_now[line] / (
                    values_now[column] * (node_points[line] - node_points[column])
                )
    matrix[0, 0] = -poly_order * (poly_order + 1) / 4.0
    matrix[7, 7] = poly_order * (poly_order + 1) / 4.0
    weights = 2.0 / (poly_order * (poly_order + 1) * values_now**2)
    return (matrix, weights)


def point_tables(full_shape, weights):
    corner_count = np.array([2.0, 1.0, 1.0, 1.0, 1.0, 1.0, 1.0, 2.0])
    weight_lines = []
    count_lines = []
    for dim_index in (1, 2, 3):
        repeats = full_shape[dim_index] // 8
        weight_lines.append(jnp.asarray(np.tile(weights, repeats), jnp.float32))
        count_lines.append(jnp.asarray(np.tile(1.0 / corner_count, repeats), jnp.float32))
    weight_cube = (
        weight_lines[0][:, None, None]
        * weight_lines[1][None, :, None]
        * weight_lines[2][None, None, :]
    )[None]
    inv_mult = (
        count_lines[0][:, None, None]
        * count_lines[1][None, :, None]
        * count_lines[2][None, None, :]
    )[None]
    return (weight_cube, inv_mult)


def derive(values, dim_index, matrix):
    full_shape = values.shape
    highest = lax.Precision.HIGHEST
    if dim_index == 1:
        blocks = values.reshape((full_shape[0], full_shape[1] // 8, 8) + full_shape[2:])
        result = jnp.einsum(
            "baipq,ji->bajpq", blocks, jnp.asarray(matrix, jnp.float32), precision=highest
        )
    elif dim_index == 2:
        blocks = values.reshape(full_shape[:2] + (full_shape[2] // 8, 8, full_shape[3]))
        result = jnp.einsum(
            "bpaiq,ji->bpajq", blocks, jnp.asarray(matrix, jnp.float32), precision=highest
        )
    else:
        block_width = math.gcd(full_shape[3], 128)
        block_matrix = jnp.asarray(np.kron(np.eye(block_width // 8), matrix), jnp.float32)
        blocks = values.reshape(full_shape[:3] + (full_shape[3] // block_width, block_width))
        result = jnp.einsum("bpqai,ji->bpqaj", blocks, block_matrix, precision=highest)
    return result.reshape(full_shape)


def gradient(values, matrix):
    return [derive(values, 1, matrix), derive(values, 2, matrix), derive(values, 3, matrix)]


def join_edges(values, upper, lower, dim_index):
    position = lax.broadcasted_iota(jnp.int32, values.shape, dim_index) % 8
    return values + jnp.where(position == 7, upper, 0.0) + jnp.where(position == 0, lower, 0.0)


def fold_faces(widened, dim_index, length):
    values = lax.slice_in_dim(widened, 1, length + 1, axis=dim_index)
    upper = lax.slice_in_dim(widened, 2, length + 2, axis=dim_index)
    lower = lax.slice_in_dim(widened, 0, length, axis=dim_index)
    return join_edges(values, upper, lower, dim_index)


def fold_local(values, dim_index):
    upper = jnp.roll(values, -1, axis=dim_index)
    lower = jnp.roll(values, 1, axis=dim_index)
    return join_edges(values, upper, lower, dim_index)


def assemble(values):
    widened = padded(values, (("dom", 1),), 1)
    values = fold_faces(widened, 1, values.shape[1])
    widened = padded(values, (("sub", 2),), 1)
    values = fold_faces(widened, 2, values.shape[2])
    return fold_local(values, 3)


def both_sums(residual, precond, applied, inv_mult):
    return lax.psum(
        (jnp.sum(residual * precond * inv_mult), jnp.sum(precond * applied * inv_mult)),
        ("dom", "sub"),
    )


def local(level_set, velocity, source):
    matrix, weights = tables()
    phase_field = level_set[None]
    weight_cube, inv_mult = point_tables(phase_field.shape, weights)
    gradients = gradient(phase_field, matrix)
    advected = phase_field - advect_step * (
        velocity[0:1] * gradients[0] + velocity[1:2] * gradients[1] + velocity[2:3] * gradients[2]
    )
    phase_field = assemble(advected) * inv_mult
    gradients = gradient(phase_field, matrix)
    magnitude = jnp.sqrt(
        gradients[0] * gradients[0] + gradients[1] * gradients[1] + gradients[2] * gradients[2]
    )
    scaled = 1.0 / jnp.maximum(magnitude, 1.0)
    normals = [gradients[0] * scaled, gradients[1] * scaled, gradients[2] * scaled]
    for sweep_index in range(SWEEPS):
        if sweep_index > 0:
            gradients = gradient(phase_field, matrix)
        compress = phase_field * (1.0 - phase_field)
        change = derive(interface_width * gradients[0] - compress * normals[0], 1, matrix)
        change = change + derive(interface_width * gradients[1] - compress * normals[1], 2, matrix)
        change = change + derive(interface_width * gradients[2] - compress * normals[2], 3, matrix)
        phase_field = phase_field + reinit_step * assemble(change) * inv_mult
    mobility = 1.0 / (1.0 + density_ratio * phase_field * phase_field)
    weighted = weight_cube * mobility
    square_t = (matrix * matrix).T
    diag_local = (
        weight_cube
        + derive(weighted, 1, square_t)
        + derive(weighted, 2, square_t)
        + derive(weighted, 3, square_t)
    )
    assembled = assemble(jnp.concatenate([weight_cube * source[None], diag_local], axis=0))
    right_side = assembled[0:1]
    diagonal = assembled[1:2]
    transposed = matrix.T

    def operate(direction):
        grads_dir = gradient(direction, matrix)
        local_sum = weight_cube * direction + derive(weighted * grads_dir[0], 1, transposed)
        local_sum = (
            local_sum
            + derive(weighted * grads_dir[1], 2, transposed)
            + derive(weighted * grads_dir[2], 3, transposed)
        )
        return assemble(local_sum)

    solution = jnp.zeros_like(right_side)
    residual = right_side
    precond = residual / diagonal
    applied = operate(precond)
    norm_now, product = both_sums(residual, precond, applied, inv_mult)
    step_size = norm_now / product
    direction = precond
    along_image = applied
    for step_index in range(PITERS):
        solution = solution + step_size * direction
        residual = residual - step_size * along_image
        if step_index + 1 < PITERS:
            precond = residual / diagonal
            applied = operate(precond)
            norm_next, product = both_sums(residual, precond, applied, inv_mult)
            ratio_new = norm_next / norm_now
            step_size = norm_next / (product - ratio_new * norm_next / step_size)
            direction = precond + ratio_new * direction
            along_image = applied + ratio_new * along_image
            norm_now = norm_next
    return (phase_field[0], solution[0], (residual / diagonal)[0])


def solution(mesh):
    return jax.shard_map(
        local,
        mesh=mesh,
        in_specs=(P("dom", "sub", None), P(None, "dom", "sub", None), P("dom", "sub", None)),
        out_specs=(P("dom", "sub", None), P("dom", "sub", None), P("dom", "sub", None)),
        check_vma=False,
    )
```

profile of v0, /device:TPU:14, one launch (start us, length us, event | category | flops | bytes accessed | tf_op | source)
XLA Modules:
  0.0 165.5 jit_solution(13758522378719981348)
XLA Ops:
  0.7 0.8 fusion.168
  1.8 0.7 copy-done
  2.8 0.6 collective-permute-start
  3.3 2.4 %collective-permute-start.1 = (f32[1,1,8,128]{3,1,2,0:T(1,128)S(1)}, f32[1,1,8,128]{3,1,2,0:T(1,128)S(1)}, u32[]{:S(2)}, u32[]{:S(2)}) collective-permute-start(f32[1,1,8,128]{3,1,2,0:T(1,128)S(1)} %get-tuple-element.74), channel_id=1, source_target_pairs={{0,4},{4,8},{8,12},{12,16},{16,20},{20,24},{24,28},{28,0},{1,5},{5... | collective-permute-start | bytes 12296 | tf_op jit(solution)/shard_map/ppermute | solution.py:33
  5.7 0.6 copy-done.10
  6.5 0.8 collective-permute-done
  7.5 0.5 collective-permute-start.3
  8.0 0.8 collective-permute-done.2
  8.8 1.8 %collective-permute-done.3 = f32[1,8,1,128]{3,1,2,0:T(8,128)S(1)} collective-permute-done((f32[1,8,1,128]{3,1,2,0:T(8,128)S(1)}, f32[1,8,1,128]{3,1,2,0:T(8,128)S(1)}, u32[]{:S(2)}, u32[]{:S(2)}) %collective-permute-start.3) | collective-permute-done | bytes 4128 | tf_op jit(solution)/shard_map/ppermute | solution.py:33
  10.8 0.7 copy-done.6
  12.8 2.0 %collective-permute-start.4 = (f32[1,1,8,128]{3,1,2,0:T(1,128)S(1)}, f32[1,1,8,128]{3,1,2,0:T(1,128)S(1)}, u32[]{:S(2)}, u32[]{:S(2)}) collective-permute-start(f32[1,1,8,128]{3,1,2,0:T(1,128)S(1)} %get-tuple-element.61), channel_id=1, source_target_pairs={{4,0},{8,4},{12,8},{16,12},{20,16},{24,20},{28,24},{0,28},{5,1},{9... | collective-permute-start | bytes 12296 | tf_op jit(solution)/shard_map/ppermute | solution.py:34
  14.8 1.1 collective-permute-start.5
  15.9 1.5 collective-permute-done.4
  17.4 1.1 collective-permute-done.5
  18.7 0.5 collective-permute-start.7
  19.2 0.8 collective-permute-done.6
  20.0 1.8 %collective-permute-done.7 = f32[1,8,1,128]{3,1,2,0:T(8,128)S(1)} collective-permute-done((f32[1,8,1,128]{3,1,2,0:T(8,128)S(1)}, f32[1,8,1,128]{3,1,2,0:T(8,128)S(1)}, u32[]{:S(2)}, u32[]{:S(2)}) %collective-permute-start.7) | collective-permute-done | bytes 4128 | tf_op jit(solution)/shard_map/ppermute | solution.py:33
  23.4 4.8 %collective-permute-start.8 = (f32[1,1,8,128]{3,1,2,0:T(1,128)S(1)}, f32[1,1,8,128]{3,1,2,0:T(1,128)S(1)}, u32[]{:S(2)}, u32[]{:S(2)}) collective-permute-start(f32[1,1,8,128]{3,1,2,0:T(1,128)S(1)} %get-tuple-element.53), channel_id=1, source_target_pairs={{4,0},{8,4},{12,8},{16,12},{20,16},{24,20},{28,24},{0,28},{5,1},{9... | collective-permute-start | bytes 12296 | tf_op jit(solution)/shard_map/ppermute | solution.py:34
  28.2 1.2 collective-permute-done.8
  29.5 2.3 %collective-permute-done.9 = f32[1,1,8,128]{3,1,2,0:T(1,128)S(1)} collective-permute-done((f32[1,1,8,128]{3,1,2,0:T(1,128)S(1)}, f32[1,1,8,128]{3,1,2,0:T(1,128)S(1)}, u32[]{:S(2)}, u32[]{:S(2)}) %collective-permute-start.9) | collective-permute-done | bytes 4128 | tf_op jit(solution)/shard_map/ppermute | solution.py:33
  32.6 0.7 collective-permute-done.10
  33.3 1.8 %collective-permute-done.11 = f32[1,8,1,128]{3,1,2,0:T(8,128)S(1)} collective-permute-done((f32[1,8,1,128]{3,1,2,0:T(8,128)S(1)}, f32[1,8,1,128]{3,1,2,0:T(8,128)S(1)}, u32[]{:S(2)}, u32[]{:S(2)}) %collective-permute-start.11) | collective-permute-done | bytes 4128 | tf_op jit(solution)/shard_map/ppermute | solution.py:33
  35.4 0.5 copy-done.8
  36.4 0.6 copy-done.11
  37.3 3.0 %collective-permute-start.12 = (f32[2,1,8,128]{3,1,2,0:T(1,128)S(1)}, f32[2,1,8,128]{3,1,2,0:T(1,128)S(1)}, u32[]{:S(2)}, u32[]{:S(2)}) collective-permute-start(f32[2,1,8,128]{3,1,2,0:T(1,128)S(1)} %get-tuple-element.29), channel_id=1, source_target_pairs={{4,0},{8,4},{12,8},{16,12},{20,16},{24,20},{28,24},{0,28},{5,1},{9... | collective-permute-start | bytes 24584 | tf_op jit(solution)/shard_map/ppermute | solution.py:34
  40.3 1.6 collective-permute-done.12
  41.9 2.0 %collective-permute-done.13 = f32[2,1,8,128]{3,1,2,0:T(1,128)S(1)} collective-permute-done((f32[2,1,8,128]{3,1,2,0:T(1,128)S(1)}, f32[2,1,8,128]{3,1,2,0:T(1,128)S(1)}, u32[]{:S(2)}, u32[]{:S(2)}) %collective-permute-start.13) | collective-permute-done | bytes 8224 | tf_op jit(solution)/shard_map/ppermute | solution.py:33
  44.1 0.5 collective-permute-start.15
  44.6 0.9 collective-permute-done.14
  45.4 1.8 %collective-permute-done.15 = f32[2,8,1,128]{3,1,2,0:T(8,128)S(1)} collective-permute-done((f32[2,8,1,128]{3,1,2,0:T(8,128)S(1)}, f32[2,8,1,128]{3,1,2,0:T(8,128)S(1)}, u32[]{:S(2)}, u32[]{:S(2)}) %collective-permute-start.15) | collective-permute-done | bytes 8224 | tf_op jit(solution)/shard_map/ppermute | solution.py:33
  48.3 0.6 copy-done.4
  49.3 0.7 copy-done.3
  50.2 2.8 %collective-permute-start.16 = (f32[1,1,8,128]{3,1,2,0:T(1,128)S(1)}, f32[1,1,8,128]{3,1,2,0:T(1,128)S(1)}, u32[]{:S(2)}, u32[]{:S(2)}) collective-permute-start(f32[1,1,8,128]{3,1,2,0:T(1,128)S(1)} %get-tuple-element.45), channel_id=1, source_target_pairs={{4,0},{8,4},{12,8},{16,12},{20,16},{24,20},{28,24},{0,28},{5,1},{9... | collective-permute-start | bytes 12296 | tf_op jit(solution)/shard_map/ppermute | solution.py:34
  53.2 1.6 collective-permute-done.16
  54.7 1.9 %collective-permute-done.17 = f32[1,1,8,128]{3,1,2,0:T(1,128)S(1)} collective-permute-done((f32[1,1,8,128]{3,1,2,0:T(1,128)S(1)}, f32[1,1,8,128]{3,1,2,0:T(1,128)S(1)}, u32[]{:S(2)}, u32[]{:S(2)}) %collective-permute-start.17) | collective-permute-done | bytes 4128 | tf_op jit(solution)/shard_map/ppermute | solution.py:33
  57.3 0.8 collective-permute-done.18
  58.1 1.8 %collective-permute-done.19 = f32[1,8,1,128]{3,1,2,0:T(8,128)S(1)} collective-permute-done((f32[1,8,1,128]{3,1,2,0:T(8,128)S(1)}, f32[1,8,1,128]{3,1,2,0:T(8,128)S(1)}, u32[]{:S(2)}, u32[]{:S(2)}) %collective-permute-start.19) | collective-permute-done | bytes 4128 | tf_op jit(solution)/shard_map/ppermute | solution.py:33
  60.1 0.7 fusion.105
  60.8 44.3 %all-reduce.1 = (f32[]{:T(128)}, f32[]{:T(128)}) all-reduce(f32[]{:T(128)} %get-tuple-element.9, f32[]{:T(128)} %get-tuple-element.8), channel_id=1, replica_groups=mesh['dom'=8,'sub'=4] {'dom','sub'}, use_global_device_ids=true, to_apply=%region_1.2 | all-reduce | flops 2 | bytes 16 | tf_op jit(solution)/shard_map/psum | solution.py:135
  107.7 0.6 collective-permute-start.20
  108.4 2.3 %collective-permute-start.21 = (f32[1,1,8,128]{3,1,2,0:T(1,128)S(1)}, f32[1,1,8,128]{3,1,2,0:T(1,128)S(1)}, u32[]{:S(2)}, u32[]{:S(2)}) collective-permute-start(f32[1,1,8,128]{3,1,2,0:T(1,128)S(1)} %get-tuple-element.38), channel_id=1, source_target_pairs={{0,4},{4,8},{8,12},{12,16},{16,20},{20,24},{24,28},{28,0},{1,5},{5... | collective-permute-start | bytes 12296 | tf_op jit(solution)/shard_map/ppermute | solution.py:33
  110.7 1.6 collective-permute-done.20
  113.0 0.6 copy.103
  113.8 1.8 %collective-permute-done.23 = f32[1,8,1,128]{3,1,2,0:T(8,128)S(1)} collective-permute-done((f32[1,8,1,128]{3,1,2,0:T(8,128)S(1)}, f32[1,8,1,128]{3,1,2,0:T(8,128)S(1)}, u32[]{:S(2)}, u32[]{:S(2)}) %collective-permute-start.23) | collective-permute-done | bytes 4128 | tf_op jit(solution)/shard_map/ppermute | solution.py:33
  115.8 0.8 fusion.107
  116.6 43.1 %all-reduce = (f32[]{:T(128)}, f32[]{:T(128)}) all-reduce(f32[]{:T(128)} %get-tuple-element.7, f32[]{:T(128)} %get-tuple-element.6), channel_id=1, replica_groups=mesh['dom'=8,'sub'=4] {'dom','sub'}, use_global_device_ids=true, to_apply=%region_5.6 | all-reduce | flops 2 | bytes 16 | tf_op jit(solution)/shard_map/psum | solution.py:135
  164.3 0.6 copy.105
  164.9 0.6 copy.104
  (120 shorter events, 11.2 us)
Async XLA Ops:
  0.6 0.8 copy-start.1
  0.6 0.8 copy-start.2
  1.6 0.9 copy-start
  2.8 4.6 %collective-permute-start = (f32[1,1,8,128]{3,1,2,0:T(1,128)S(1)}, f32[1,1,8,128]{3,1,2,0:T(1,128)S(1)}, u32[]{:S(2)}, u32[]{:S(2)}) collective-permute-start(f32[1,1,8,128]{3,1,2,0:T(1,128)S(1)} %get-tuple-element.73), channel_id=1, source_target_pairs={{4,0},{8,4},{12,8},{16,12},{20,16},{24,20},{28,24},{0,28},{5,1},{9... | collective-permute-start | bytes 12296 | tf_op jit(solution)/shard_map/ppermute | solution.py:34
  3.3 4.0 %collective-permute-start.1 = (f32[1,1,8,128]{3,1,2,0:T(1,128)S(1)}, f32[1,1,8,128]{3,1,2,0:T(1,128)S(1)}, u32[]{:S(2)}, u32[]{:S(2)}) collective-permute-start(f32[1,1,8,128]{3,1,2,0:T(1,128)S(1)} %get-tuple-element.74), channel_id=1, source_target_pairs={{0,4},{4,8},{8,12},{12,16},{16,20},{20,24},{24,28},{28,0},{1,5},{5... | collective-permute-start | bytes 12296 | tf_op jit(solution)/shard_map/ppermute | solution.py:33
  5.7 0.7 copy-start.10
  7.4 1.4 collective-permute-start.2
  7.5 3.1 %collective-permute-start.3 = (f32[1,8,1,128]{3,1,2,0:T(8,128)S(1)}, f32[1,8,1,128]{3,1,2,0:T(8,128)S(1)}, u32[]{:S(2)}, u32[]{:S(2)}) collective-permute-start(f32[1,8,1,128]{3,1,2,0:T(8,128)S(1)} %get-tuple-element.72), channel_id=1, source_target_pairs={{0,1},{1,2},{2,3},{3,0},{4,5},{5,6},{6,7},{7,4},{8,9},{9,10},{10,1... | collective-permute-start | bytes 12296 | tf_op jit(solution)/shard_map/ppermute | solution.py:33
  10.8 0.7 copy-start.6
  12.8 4.6 %collective-permute-start.4 = (f32[1,1,8,128]{3,1,2,0:T(1,128)S(1)}, f32[1,1,8,128]{3,1,2,0:T(1,128)S(1)}, u32[]{:S(2)}, u32[]{:S(2)}) collective-permute-start(f32[1,1,8,128]{3,1,2,0:T(1,128)S(1)} %get-tuple-element.61), channel_id=1, source_target_pairs={{4,0},{8,4},{12,8},{16,12},{20,16},{24,20},{28,24},{0,28},{5,1},{9... | collective-permute-start | bytes 12296 | tf_op jit(solution)/shard_map/ppermute | solution.py:34
  14.8 3.7 %collective-permute-start.5 = (f32[1,1,8,128]{3,1,2,0:T(1,128)S(1)}, f32[1,1,8,128]{3,1,2,0:T(1,128)S(1)}, u32[]{:S(2)}, u32[]{:S(2)}) collective-permute-start(f32[1,1,8,128]{3,1,2,0:T(1,128)S(1)} %get-tuple-element.62), channel_id=1, source_target_pairs={{0,4},{4,8},{8,12},{12,16},{16,20},{20,24},{24,28},{28,0},{1,5},{5... | collective-permute-start | bytes 12296 | tf_op jit(solution)/shard_map/ppermute | solution.py:33
  18.6 1.4 collective-permute-start.6
  18.7 3.1 %collective-permute-start.7 = (f32[1,8,1,128]{3,1,2,0:T(8,128)S(1)}, f32[1,8,1,128]{3,1,2,0:T(8,128)S(1)}, u32[]{:S(2)}, u32[]{:S(2)}) collective-permute-start(f32[1,8,1,128]{3,1,2,0:T(8,128)S(1)} %get-tuple-element.60), channel_id=1, source_target_pairs={{0,1},{1,2},{2,3},{3,0},{4,5},{5,6},{6,7},{7,4},{8,9},{9,10},{10,1... | collective-permute-start | bytes 12296 | tf_op jit(solution)/shard_map/ppermute | solution.py:33
  23.4 4.8 %copy-start.9 = (f32[8]{0:T(128)S(1)}, f32[8]{0:T(128)}, u32[]{:S(2)}) copy-start(f32[8]{0:T(128)} %constant.109.clone) | copy-start | bytes 100
  23.4 6.1 %collective-permute-start.8 = (f32[1,1,8,128]{3,1,2,0:T(1,128)S(1)}, f32[1,1,8,128]{3,1,2,0:T(1,128)S(1)}, u32[]{:S(2)}, u32[]{:S(2)}) collective-permute-start(f32[1,1,8,128]{3,1,2,0:T(1,128)S(1)} %get-tuple-element.53), channel_id=1, source_target_pairs={{4,0},{8,4},{12,8},{16,12},{20,16},{24,20},{28,24},{0,28},{5,1},{9... | collective-permute-start | bytes 12296 | tf_op jit(solution)/shard_map/ppermute | solution.py:34
  28.2 3.6 %collective-permute-start.9 = (f32[1,1,8,128]{3,1,2,0:T(1,128)S(1)}, f32[1,1,8,128]{3,1,2,0:T(1,128)S(1)}, u32[]{:S(2)}, u32[]{:S(2)}) collective-permute-start(f32[1,1,8,128]{3,1,2,0:T(1,128)S(1)} %get-tuple-element.54), channel_id=1, source_target_pairs={{0,4},{4,8},{8,12},{12,16},{16,20},{20,24},{24,28},{28,0},{1,5},{5... | collective-permute-start | bytes 12296 | tf_op jit(solution)/shard_map/ppermute | solution.py:33
  28.2 4.2 %copy-start.5 = (f32[8,8,128]{2,1,0:T(8,128)S(1)}, f32[8,8,128]{2,1,0:T(8,128)}, u32[]{:S(2)}) copy-start(f32[8,8,128]{2,1,0:T(8,128)} %param.41) | copy-start | bytes 98308
  31.9 0.7 copy-start.7
  31.9 1.4 collective-permute-start.10
  31.9 3.1 %collective-permute-start.11 = (f32[1,8,1,128]{3,1,2,0:T(8,128)S(1)}, f32[1,8,1,128]{3,1,2,0:T(8,128)S(1)}, u32[]{:S(2)}, u32[]{:S(2)}) collective-permute-start(f32[1,8,1,128]{3,1,2,0:T(8,128)S(1)} %get-tuple-element.52), channel_id=1, source_target_pairs={{0,1},{1,2},{2,3},{3,0},{4,5},{5,6},{6,7},{7,4},{8,9},{9,10},{10,1... | collective-permute-start | bytes 12296 | tf_op jit(solution)/shard_map/ppermute | solution.py:33
  35.3 0.7 copy-start.8
  36.1 0.9 copy-start.11
  37.3 4.6 %collective-permute-start.12 = (f32[2,1,8,128]{3,1,2,0:T(1,128)S(1)}, f32[2,1,8,128]{3,1,2,0:T(1,128)S(1)}, u32[]{:S(2)}, u32[]{:S(2)}) collective-permute-start(f32[2,1,8,128]{3,1,2,0:T(1,128)S(1)} %get-tuple-element.29), channel_id=1, source_target_pairs={{4,0},{8,4},{12,8},{16,12},{20,16},{24,20},{28,24},{0,28},{5,1},{9... | collective-permute-start | bytes 24584 | tf_op jit(solution)/shard_map/ppermute | solution.py:34
  40.3 3.7 %collective-permute-start.13 = (f32[2,1,8,128]{3,1,2,0:T(1,128)S(1)}, f32[2,1,8,128]{3,1,2,0:T(1,128)S(1)}, u32[]{:S(2)}, u32[]{:S(2)}) collective-permute-start(f32[2,1,8,128]{3,1,2,0:T(1,128)S(1)} %get-tuple-element.30), channel_id=1, source_target_pairs={{0,4},{4,8},{8,12},{12,16},{16,20},{20,24},{24,28},{28,0},{1,5},{5... | collective-permute-start | bytes 24584 | tf_op jit(solution)/shard_map/ppermute | solution.py:33
  44.0 1.4 collective-permute-start.14
  44.1 3.1 %collective-permute-start.15 = (f32[2,8,1,128]{3,1,2,0:T(8,128)S(1)}, f32[2,8,1,128]{3,1,2,0:T(8,128)S(1)}, u32[]{:S(2)}, u32[]{:S(2)}) collective-permute-start(f32[2,8,1,128]{3,1,2,0:T(8,128)S(1)} %get-tuple-element.28), channel_id=1, source_target_pairs={{0,1},{1,2},{2,3},{3,0},{4,5},{5,6},{6,7},{7,4},{8,9},{9,10},{10,1... | collective-permute-start | bytes 24584 | tf_op jit(solution)/shard_map/ppermute | solution.py:33
  48.2 0.7 copy-start.4
  49.1 0.8 copy-start.3
  50.2 4.6 %collective-permute-start.16 = (f32[1,1,8,128]{3,1,2,0:T(1,128)S(1)}, f32[1,1,8,128]{3,1,2,0:T(1,128)S(1)}, u32[]{:S(2)}, u32[]{:S(2)}) collective-permute-start(f32[1,1,8,128]{3,1,2,0:T(1,128)S(1)} %get-tuple-element.45), channel_id=1, source_target_pairs={{4,0},{8,4},{12,8},{16,12},{20,16},{24,20},{28,24},{0,28},{5,1},{9... | collective-permute-start | bytes 12296 | tf_op jit(solution)/shard_map/ppermute | solution.py:34
  53.0 3.6 %collective-permute-start.17 = (f32[1,1,8,128]{3,1,2,0:T(1,128)S(1)}, f32[1,1,8,128]{3,1,2,0:T(1,128)S(1)}, u32[]{:S(2)}, u32[]{:S(2)}) collective-permute-start(f32[1,1,8,128]{3,1,2,0:T(1,128)S(1)} %get-tuple-element.46), channel_id=1, source_target_pairs={{0,4},{4,8},{8,12},{12,16},{16,20},{20,24},{24,28},{28,0},{1,5},{5... | collective-permute-start | bytes 12296 | tf_op jit(solution)/shard_map/ppermute | solution.py:33
  56.7 1.4 collective-permute-start.18
  56.8 3.1 %collective-permute-start.19 = (f32[1,8,1,128]{3,1,2,0:T(8,128)S(1)}, f32[1,8,1,128]{3,1,2,0:T(8,128)S(1)}, u32[]{:S(2)}, u32[]{:S(2)}) collective-permute-start(f32[1,8,1,128]{3,1,2,0:T(8,128)S(1)} %get-tuple-element.44), channel_id=1, source_target_pairs={{0,1},{1,2},{2,3},{3,0},{4,5},{5,6},{6,7},{7,4},{8,9},{9,10},{10,1... | collective-permute-start | bytes 12296 | tf_op jit(solution)/shard_map/ppermute | solution.py:33
  107.7 4.6 %collective-permute-start.20 = (f32[1,1,8,128]{3,1,2,0:T(1,128)S(1)}, f32[1,1,8,128]{3,1,2,0:T(1,128)S(1)}, u32[]{:S(2)}, u32[]{:S(2)}) collective-permute-start(f32[1,1,8,128]{3,1,2,0:T(1,128)S(1)} %get-tuple-element.37), channel_id=1, source_target_pairs={{4,0},{8,4},{12,8},{16,12},{20,16},{24,20},{28,24},{0,28},{5,1},{9... | collective-permute-start | bytes 12296 | tf_op jit(solution)/shard_map/ppermute | solution.py:34
  108.4 3.9 %collective-permute-start.21 = (f32[1,1,8,128]{3,1,2,0:T(1,128)S(1)}, f32[1,1,8,128]{3,1,2,0:T(1,128)S(1)}, u32[]{:S(2)}, u32[]{:S(2)}) collective-permute-start(f32[1,1,8,128]{3,1,2,0:T(1,128)S(1)} %get-tuple-element.38), channel_id=1, source_target_pairs={{0,4},{4,8},{8,12},{12,16},{16,20},{20,24},{24,28},{28,0},{1,5},{5... | collective-permute-start | bytes 12296 | tf_op jit(solution)/shard_map/ppermute | solution.py:33
  112.4 1.4 collective-permute-start.22
  112.5 3.1 %collective-permute-start.23 = (f32[1,8,1,128]{3,1,2,0:T(8,128)S(1)}, f32[1,8,1,128]{3,1,2,0:T(8,128)S(1)}, u32[]{:S(2)}, u32[]{:S(2)}) collective-permute-start(f32[1,8,1,128]{3,1,2,0:T(8,128)S(1)} %get-tuple-element.36), channel_id=1, source_target_pairs={{0,1},{1,2},{2,3},{3,0},{4,5},{5,6},{6,7},{7,4},{8,9},{9,10},{10,1... | collective-permute-start | bytes 12296 | tf_op jit(solution)/shard_map/ppermute | solution.py:33
where the time goes:
time: 166 us
  blocking collectives  87.4 us (53%)
  waiting for transfers between devices  30.5 us (18%)
  starting transfers between devices  23.1 us (14%)
  local copies, waits for them, and re-layouts  8.16 us (5%)
  between operations  7.03 us (4%)
  matrix products  5.75 us (3%)
  other arithmetic  3.65 us (2%)
    psum x2, blocking collectives, both_sums(): lax.psum((jnp.sum(residual * precond * inv_mult), jnp.sum(precond * appli...  87.4 us
    ppermute x12, waiting for transfers between devices, padded(): before = lax.ppermute(last, axis, up)  17.9 us
    ppermute x12, starting transfers between devices, padded(): after = lax.ppermute(leading, axis, down)  14.1 us
    ppermute x12, waiting for transfers between devices, padded(): after = lax.ppermute(leading, axis, down)  12.6 us
    ppermute x12, starting transfers between devices, padded(): before = lax.ppermute(last, axis, up)  8.96 us
    unnamed x27, local copies, waits for them, and re-layouts  6.39 us
  transfers between devices with their start and end apart: 24, of which 22 were waited for; matrix products, arithmetic and copies ran while one was open for 1% of the time, Pallas kernels for 0%

commit v1 on v0

--- a/solution.py
+++ b/solution.py
@@ -133,8 +133,11 @@
 
 def both_sums(residual, precond, applied, inv_mult):
     return lax.psum(
-        (jnp.sum(residual * precond * inv_mult), jnp.sum(precond * applied * inv_mult)),
-        ("dom", "sub"),
+        lax.psum(
+            (jnp.sum(residual * precond * inv_mult), jnp.sum(precond * applied * inv_mult)),
+            axis_name="sub",
+        ),
+        axis_name="dom",
     )
 
 

time: 166 us -> 137 us (0.83)
  the two profiles are of different devices: /device:TPU:14 before, /device:TPU:0 now
where the time goes in v1:
time: 137 us
  blocking collectives  48.3 us (35%)
  waiting for transfers between devices  44.1 us (32%)
  starting transfers between devices  19.8 us (14%)
  local copies, waits for them, and re-layouts  8.15 us (6%)
  between operations  7.11 us (5%)
  matrix products  5.75 us (4%)
  other arithmetic  3.64 us (3%)
    psum x2, blocking collectives, both_sums(): lax.psum(lax.psum((jnp.sum(residual * precond * inv_mult), jnp.sum(precon...  35.6 us
    ppermute x12, waiting for transfers between devices, padded(): before = lax.ppermute(last, axis, up)  31.5 us
    psum x2, blocking collectives, both_sums(): lax.psum((jnp.sum(residual * precond * inv_mult), jnp.sum(precond * appli...  12.7 us
    ppermute x12, waiting for transfers between devices, padded(): after = lax.ppermute(leading, axis, down)  12.6 us
    ppermute x12, starting transfers between devices, padded(): before = lax.ppermute(last, axis, up)  11.1 us
    ppermute x12, starting transfers between devices, padded(): after = lax.ppermute(leading, axis, down)  8.7 us
    unnamed x27, local copies, waits for them, and re-layouts  6.38 us
  transfers between devices with their start and end apart: 24, of which 24 were waited for; matrix products, arithmetic and copies ran while one was open for 1% of the time, Pallas kernels for 0%

profile of v1, /device:TPU:0, one launch (start us, length us, event | category | flops | bytes accessed | tf_op | source)
XLA Modules:
  0.0 136.8 jit_solution(3530592171231972930)
XLA Ops:
  0.7 0.8 fusion.168
  1.8 0.7 copy-done
  2.7 6.1 %collective-permute-start = (f32[1,1,8,128]{3,1,2,0:T(1,128)S(1)}, f32[1,1,8,128]{3,1,2,0:T(1,128)S(1)}, u32[]{:S(2)}, u32[]{:S(2)}) collective-permute-start(f32[1,1,8,128]{3,1,2,0:T(1,128)S(1)} %get-tuple-element.77), channel_id=1, source_target_pairs={{4,0},{8,4},{12,8},{16,12},{20,16},{24,20},{28,24},{0,28},{5,1},{9... | collective-permute-start | bytes 12296 | tf_op jit(solution)/shard_map/ppermute | solution.py:34
  8.8 0.6 copy-done.10
  9.6 0.6 collective-permute-done
  10.1 5.0 %collective-permute-done.1 = f32[1,1,8,128]{3,1,2,0:T(1,128)S(1)} collective-permute-done((f32[1,1,8,128]{3,1,2,0:T(1,128)S(1)}, f32[1,1,8,128]{3,1,2,0:T(1,128)S(1)}, u32[]{:S(2)}, u32[]{:S(2)}) %collective-permute-start.1) | collective-permute-done | bytes 4128 | tf_op jit(solution)/shard_map/ppermute | solution.py:33
  15.8 0.8 collective-permute-done.2
  16.6 1.8 %collective-permute-done.3 = f32[1,8,1,128]{3,1,2,0:T(8,128)S(1)} collective-permute-done((f32[1,8,1,128]{3,1,2,0:T(8,128)S(1)}, f32[1,8,1,128]{3,1,2,0:T(8,128)S(1)}, u32[]{:S(2)}, u32[]{:S(2)}) %collective-permute-start.3) | collective-permute-done | bytes 4128 | tf_op jit(solution)/shard_map/ppermute | solution.py:33
  18.6 0.7 copy-done.6
  20.7 2.0 %collective-permute-start.5 = (f32[1,1,8,128]{3,1,2,0:T(1,128)S(1)}, f32[1,1,8,128]{3,1,2,0:T(1,128)S(1)}, u32[]{:S(2)}, u32[]{:S(2)}) collective-permute-start(f32[1,1,8,128]{3,1,2,0:T(1,128)S(1)} %get-tuple-element.66), channel_id=1, source_target_pairs={{0,4},{4,8},{8,12},{12,16},{16,20},{20,24},{24,28},{28,0},{1,5},{5... | collective-permute-start | bytes 12296 | tf_op jit(solution)/shard_map/ppermute | solution.py:33
  22.8 1.6 %collective-permute-done.4 = f32[1,1,8,128]{3,1,2,0:T(1,128)S(1)} collective-permute-done((f32[1,1,8,128]{3,1,2,0:T(1,128)S(1)}, f32[1,1,8,128]{3,1,2,0:T(1,128)S(1)}, u32[]{:S(2)}, u32[]{:S(2)}) %collective-permute-start.4) | collective-permute-done | bytes 4128 | tf_op jit(solution)/shard_map/ppermute | solution.py:34
  24.3 2.8 %collective-permute-done.5 = f32[1,1,8,128]{3,1,2,0:T(1,128)S(1)} collective-permute-done((f32[1,1,8,128]{3,1,2,0:T(1,128)S(1)}, f32[1,1,8,128]{3,1,2,0:T(1,128)S(1)}, u32[]{:S(2)}, u32[]{:S(2)}) %collective-permute-start.5) | collective-permute-done | bytes 4128 | tf_op jit(solution)/shard_map/ppermute | solution.py:33
  27.3 0.5 collective-permute-start.7
  27.7 0.8 collective-permute-done.6
  28.6 1.8 %collective-permute-done.7 = f32[1,8,1,128]{3,1,2,0:T(8,128)S(1)} collective-permute-done((f32[1,8,1,128]{3,1,2,0:T(8,128)S(1)}, f32[1,8,1,128]{3,1,2,0:T(8,128)S(1)}, u32[]{:S(2)}, u32[]{:S(2)}) %collective-permute-start.7) | collective-permute-done | bytes 4128 | tf_op jit(solution)/shard_map/ppermute | solution.py:33
  32.1 2.0 %collective-permute-start.9 = (f32[1,1,8,128]{3,1,2,0:T(1,128)S(1)}, f32[1,1,8,128]{3,1,2,0:T(1,128)S(1)}, u32[]{:S(2)}, u32[]{:S(2)}) collective-permute-start(f32[1,1,8,128]{3,1,2,0:T(1,128)S(1)} %get-tuple-element.58), channel_id=1, source_target_pairs={{0,4},{4,8},{8,12},{12,16},{16,20},{20,24},{24,28},{28,0},{1,5},{5... | collective-permute-start | bytes 12296 | tf_op jit(solution)/shard_map/ppermute | solution.py:33
  34.1 1.5 %collective-permute-done.8 = f32[1,1,8,128]{3,1,2,0:T(1,128)S(1)} collective-permute-done((f32[1,1,8,128]{3,1,2,0:T(1,128)S(1)}, f32[1,1,8,128]{3,1,2,0:T(1,128)S(1)}, u32[]{:S(2)}, u32[]{:S(2)}) %collective-permute-start.8) | collective-permute-done | bytes 4128 | tf_op jit(solution)/shard_map/ppermute | solution.py:34
  35.6 2.8 %collective-permute-done.9 = f32[1,1,8,128]{3,1,2,0:T(1,128)S(1)} collective-permute-done((f32[1,1,8,128]{3,1,2,0:T(1,128)S(1)}, f32[1,1,8,128]{3,1,2,0:T(1,128)S(1)}, u32[]{:S(2)}, u32[]{:S(2)}) %collective-permute-start.9) | collective-permute-done | bytes 4128 | tf_op jit(solution)/shard_map/ppermute | solution.py:33
  39.2 0.7 collective-permute-done.10
  39.9 1.8 %collective-permute-done.11 = f32[1,8,1,128]{3,1,2,0:T(8,128)S(1)} collective-permute-done((f32[1,8,1,128]{3,1,2,0:T(8,128)S(1)}, f32[1,8,1,128]{3,1,2,0:T(8,128)S(1)}, u32[]{:S(2)}, u32[]{:S(2)}) %collective-permute-start.11) | collective-permute-done | bytes 4128 | tf_op jit(solution)/shard_map/ppermute | solution.py:33
  42.1 0.5 copy-done.8
  43.0 0.6 copy-done.11
  44.0 2.0 %collective-permute-start.13 = (f32[2,1,8,128]{3,1,2,0:T(1,128)S(1)}, f32[2,1,8,128]{3,1,2,0:T(1,128)S(1)}, u32[]{:S(2)}, u32[]{:S(2)}) collective-permute-start(f32[2,1,8,128]{3,1,2,0:T(1,128)S(1)} %get-tuple-element.34), channel_id=1, source_target_pairs={{0,4},{4,8},{8,12},{12,16},{16,20},{20,24},{24,28},{28,0},{1,5},{5... | collective-permute-start | bytes 24584 | tf_op jit(solution)/shard_map/ppermute | solution.py:33
  46.0 1.6 %collective-permute-done.12 = f32[2,1,8,128]{3,1,2,0:T(1,128)S(1)} collective-permute-done((f32[2,1,8,128]{3,1,2,0:T(1,128)S(1)}, f32[2,1,8,128]{3,1,2,0:T(1,128)S(1)}, u32[]{:S(2)}, u32[]{:S(2)}) %collective-permute-start.12) | collective-permute-done | bytes 8224 | tf_op jit(solution)/shard_map/ppermute | solution.py:34
  47.6 2.8 %collective-permute-done.13 = f32[2,1,8,128]{3,1,2,0:T(1,128)S(1)} collective-permute-done((f32[2,1,8,128]{3,1,2,0:T(1,128)S(1)}, f32[2,1,8,128]{3,1,2,0:T(1,128)S(1)}, u32[]{:S(2)}, u32[]{:S(2)}) %collective-permute-start.13) | collective-permute-done | bytes 8224 | tf_op jit(solution)/shard_map/ppermute | solution.py:33
  51.0 0.9 collective-permute-done.14
  51.9 1.8 %collective-permute-done.15 = f32[2,8,1,128]{3,1,2,0:T(8,128)S(1)} collective-permute-done((f32[2,8,1,128]{3,1,2,0:T(8,128)S(1)}, f32[2,8,1,128]{3,1,2,0:T(8,128)S(1)}, u32[]{:S(2)}, u32[]{:S(2)}) %collective-permute-start.15) | collective-permute-done | bytes 8224 | tf_op jit(solution)/shard_map/ppermute | solution.py:33
  54.8 0.6 copy-done.4
  55.8 0.7 copy-done.3
  56.8 2.0 %collective-permute-start.17 = (f32[1,1,8,128]{3,1,2,0:T(1,128)S(1)}, f32[1,1,8,128]{3,1,2,0:T(1,128)S(1)}, u32[]{:S(2)}, u32[]{:S(2)}) collective-permute-start(f32[1,1,8,128]{3,1,2,0:T(1,128)S(1)} %get-tuple-element.50), channel_id=1, source_target_pairs={{0,4},{4,8},{8,12},{12,16},{16,20},{20,24},{24,28},{28,0},{1,5},{5... | collective-permute-start | bytes 12296 | tf_op jit(solution)/shard_map/ppermute | solution.py:33
  58.8 1.6 %collective-permute-done.16 = f32[1,1,8,128]{3,1,2,0:T(1,128)S(1)} collective-permute-done((f32[1,1,8,128]{3,1,2,0:T(1,128)S(1)}, f32[1,1,8,128]{3,1,2,0:T(1,128)S(1)}, u32[]{:S(2)}, u32[]{:S(2)}) %collective-permute-start.16) | collective-permute-done | bytes 4128 | tf_op jit(solution)/shard_map/ppermute | solution.py:34
  60.4 2.8 %collective-permute-done.17 = f32[1,1,8,128]{3,1,2,0:T(1,128)S(1)} collective-permute-done((f32[1,1,8,128]{3,1,2,0:T(1,128)S(1)}, f32[1,1,8,128]{3,1,2,0:T(1,128)S(1)}, u32[]{:S(2)}, u32[]{:S(2)}) %collective-permute-start.17) | collective-permute-done | bytes 4128 | tf_op jit(solution)/shard_map/ppermute | solution.py:33
  63.8 0.8 collective-permute-done.18
  64.6 1.8 %collective-permute-done.19 = f32[1,8,1,128]{3,1,2,0:T(8,128)S(1)} collective-permute-done((f32[1,8,1,128]{3,1,2,0:T(8,128)S(1)}, f32[1,8,1,128]{3,1,2,0:T(8,128)S(1)}, u32[]{:S(2)}, u32[]{:S(2)}) %collective-permute-start.19) | collective-permute-done | bytes 4128 | tf_op jit(solution)/shard_map/ppermute | solution.py:33
  66.6 0.7 fusion.105
  67.3 6.3 %all-reduce.3 = (f32[]{:T(128)}, f32[]{:T(128)}) all-reduce(f32[]{:T(128)} %get-tuple-element.9, f32[]{:T(128)} %get-tuple-element.8), channel_id=1, replica_groups=mesh['dom'=8,'sub'=4] {'sub'}, use_global_device_ids=true, to_apply=%region_1.2 | all-reduce | flops 2 | bytes 16 | tf_op jit(solution)/shard_map/psum | solution.py:136
  73.6 17.8 %all-reduce.1 = (f32[]{:T(128)}, f32[]{:T(128)}) all-reduce(f32[]{:T(128)} %get-tuple-element.16, f32[]{:T(128)} %get-tuple-element.17), channel_id=1, replica_groups=mesh['dom'=8,'sub'=4] {'dom'}, use_global_device_ids=true, to_apply=%region_2.3 | all-reduce | flops 2 | bytes 16 | tf_op jit(solution)/shard_map/psum | solution.py:135
  94.0 2.1 %collective-permute-start.20 = (f32[1,1,8,128]{3,1,2,0:T(1,128)S(1)}, f32[1,1,8,128]{3,1,2,0:T(1,128)S(1)}, u32[]{:S(2)}, u32[]{:S(2)}) collective-permute-start(f32[1,1,8,128]{3,1,2,0:T(1,128)S(1)} %get-tuple-element.41), channel_id=1, source_target_pairs={{4,0},{8,4},{12,8},{16,12},{20,16},{24,20},{28,24},{0,28},{5,1},{9... | collective-permute-start | bytes 12296 | tf_op jit(solution)/shard_map/ppermute | solution.py:34
  96.1 1.5 %collective-permute-done.20 = f32[1,1,8,128]{3,1,2,0:T(1,128)S(1)} collective-permute-done((f32[1,1,8,128]{3,1,2,0:T(1,128)S(1)}, f32[1,1,8,128]{3,1,2,0:T(1,128)S(1)}, u32[]{:S(2)}, u32[]{:S(2)}) %collective-permute-start.20) | collective-permute-done | bytes 4128 | tf_op jit(solution)/shard_map/ppermute | solution.py:34
  97.7 4.7 %collective-permute-done.21 = f32[1,1,8,128]{3,1,2,0:T(1,128)S(1)} collective-permute-done((f32[1,1,8,128]{3,1,2,0:T(1,128)S(1)}, f32[1,1,8,128]{3,1,2,0:T(1,128)S(1)}, u32[]{:S(2)}, u32[]{:S(2)}) %collective-permute-start.21) | collective-permute-done | bytes 4128 | tf_op jit(solution)/shard_map/ppermute | solution.py:33
  102.5 0.5 collective-permute-start.23
  103.0 0.6 copy.103
  103.8 1.8 %collective-permute-done.23 = f32[1,8,1,128]{3,1,2,0:T(8,128)S(1)} collective-permute-done((f32[1,8,1,128]{3,1,2,0:T(8,128)S(1)}, f32[1,8,1,128]{3,1,2,0:T(8,128)S(1)}, u32[]{:S(2)}, u32[]{:S(2)}) %collective-permute-start.23) | collective-permute-done | bytes 4128 | tf_op jit(solution)/shard_map/ppermute | solution.py:33
  105.9 0.8 fusion.107
  106.7 6.4 %all-reduce.2 = (f32[]{:T(128)}, f32[]{:T(128)}) all-reduce(f32[]{:T(128)} %get-tuple-element.7, f32[]{:T(128)} %get-tuple-element.6), channel_id=1, replica_groups=mesh['dom'=8,'sub'=4] {'sub'}, use_global_device_ids=true, to_apply=%region_7.8 | all-reduce | flops 2 | bytes 16 | tf_op jit(solution)/shard_map/psum | solution.py:136
  113.1 17.8 %all-reduce = (f32[]{:T(128)}, f32[]{:T(128)}) all-reduce(f32[]{:T(128)} %get-tuple-element.14, f32[]{:T(128)} %get-tuple-element.15), channel_id=1, replica_groups=mesh['dom'=8,'sub'=4] {'dom'}, use_global_device_ids=true, to_apply=%region_8.9 | all-reduce | flops 2 | bytes 16 | tf_op jit(solution)/shard_map/psum | solution.py:135
  135.6 0.6 copy.105
  136.2 0.6 copy.104
  (122 shorter events, 11.8 us)
Async XLA Ops:
  0.6 0.8 copy-start.1
  0.6 0.8 copy-start.2
  1.6 0.8 copy-start
  2.7 7.4 %collective-permute-start = (f32[1,1,8,128]{3,1,2,0:T(1,128)S(1)}, f32[1,1,8,128]{3,1,2,0:T(1,128)S(1)}, u32[]{:S(2)}, u32[]{:S(2)}) collective-permute-start(f32[1,1,8,128]{3,1,2,0:T(1,128)S(1)} %get-tuple-element.77), channel_id=1, source_target_pairs={{4,0},{8,4},{12,8},{16,12},{20,16},{24,20},{28,24},{0,28},{5,1},{9... | collective-permute-start | bytes 12296 | tf_op jit(solution)/shard_map/ppermute | solution.py:34
  8.8 6.3 %collective-permute-start.1 = (f32[1,1,8,128]{3,1,2,0:T(1,128)S(1)}, f32[1,1,8,128]{3,1,2,0:T(1,128)S(1)}, u32[]{:S(2)}, u32[]{:S(2)}) collective-permute-start(f32[1,1,8,128]{3,1,2,0:T(1,128)S(1)} %get-tuple-element.78), channel_id=1, source_target_pairs={{0,4},{4,8},{8,12},{12,16},{16,20},{20,24},{24,28},{28,0},{1,5},{5... | collective-permute-start | bytes 12296 | tf_op jit(solution)/shard_map/ppermute | solution.py:33
  8.8 0.7 copy-start.10
  15.2 1.4 %collective-permute-start.2 = (f32[1,8,1,128]{3,1,2,0:T(8,128)S(1)}, f32[1,8,1,128]{3,1,2,0:T(8,128)S(1)}, u32[]{:S(2)}, u32[]{:S(2)}) collective-permute-start(f32[1,8,1,128]{3,1,2,0:T(8,128)S(1)} %get-tuple-element.75), channel_id=1, source_target_pairs={{1,0},{2,1},{3,2},{0,3},{5,4},{6,5},{7,6},{4,7},{9,8},{10,9},{11,1... | collective-permute-start | bytes 12296 | tf_op jit(solution)/shard_map/ppermute | solution.py:34
  15.3 3.1 %collective-permute-start.3 = (f32[1,8,1,128]{3,1,2,0:T(8,128)S(1)}, f32[1,8,1,128]{3,1,2,0:T(8,128)S(1)}, u32[]{:S(2)}, u32[]{:S(2)}) collective-permute-start(f32[1,8,1,128]{3,1,2,0:T(8,128)S(1)} %get-tuple-element.76), channel_id=1, source_target_pairs={{0,1},{1,2},{2,3},{3,0},{4,5},{5,6},{6,7},{7,4},{8,9},{9,10},{10,1... | collective-permute-start | bytes 12296 | tf_op jit(solution)/shard_map/ppermute | solution.py:33
  18.6 0.7 copy-start.6
  20.7 3.7 %collective-permute-start.4 = (f32[1,1,8,128]{3,1,2,0:T(1,128)S(1)}, f32[1,1,8,128]{3,1,2,0:T(1,128)S(1)}, u32[]{:S(2)}, u32[]{:S(2)}) collective-permute-start(f32[1,1,8,128]{3,1,2,0:T(1,128)S(1)} %get-tuple-element.65), channel_id=1, source_target_pairs={{4,0},{8,4},{12,8},{16,12},{20,16},{24,20},{28,24},{0,28},{5,1},{9... | collective-permute-start | bytes 12296 | tf_op jit(solution)/shard_map/ppermute | solution.py:34
  20.7 6.4 %collective-permute-start.5 = (f32[1,1,8,128]{3,1,2,0:T(1,128)S(1)}, f32[1,1,8,128]{3,1,2,0:T(1,128)S(1)}, u32[]{:S(2)}, u32[]{:S(2)}) collective-permute-start(f32[1,1,8,128]{3,1,2,0:T(1,128)S(1)} %get-tuple-element.66), channel_id=1, source_target_pairs={{0,4},{4,8},{8,12},{12,16},{16,20},{20,24},{24,28},{28,0},{1,5},{5... | collective-permute-start | bytes 12296 | tf_op jit(solution)/shard_map/ppermute | solution.py:33
  27.2 1.4 %collective-permute-start.6 = (f32[1,8,1,128]{3,1,2,0:T(8,128)S(1)}, f32[1,8,1,128]{3,1,2,0:T(8,128)S(1)}, u32[]{:S(2)}, u32[]{:S(2)}) collective-permute-start(f32[1,8,1,128]{3,1,2,0:T(8,128)S(1)} %get-tuple-element.63), channel_id=1, source_target_pairs={{1,0},{2,1},{3,2},{0,3},{5,4},{6,5},{7,6},{4,7},{9,8},{10,9},{11,1... | collective-permute-start | bytes 12296 | tf_op jit(solution)/shard_map/ppermute | solution.py:34
  27.3 3.1 %collective-permute-start.7 = (f32[1,8,1,128]{3,1,2,0:T(8,128)S(1)}, f32[1,8,1,128]{3,1,2,0:T(8,128)S(1)}, u32[]{:S(2)}, u32[]{:S(2)}) collective-permute-start(f32[1,8,1,128]{3,1,2,0:T(8,128)S(1)} %get-tuple-element.64), channel_id=1, source_target_pairs={{0,1},{1,2},{2,3},{3,0},{4,5},{5,6},{6,7},{7,4},{8,9},{9,10},{10,1... | collective-permute-start | bytes 12296 | tf_op jit(solution)/shard_map/ppermute | solution.py:33
  32.0 2.1 %copy-start.9 = (f32[8]{0:T(128)S(1)}, f32[8]{0:T(128)}, u32[]{:S(2)}) copy-start(f32[8]{0:T(128)} %constant.109.clone) | copy-start | bytes 100
  32.0 3.7 %collective-permute-start.8 = (f32[1,1,8,128]{3,1,2,0:T(1,128)S(1)}, f32[1,1,8,128]{3,1,2,0:T(1,128)S(1)}, u32[]{:S(2)}, u32[]{:S(2)}) collective-permute-start(f32[1,1,8,128]{3,1,2,0:T(1,128)S(1)} %get-tuple-element.57), channel_id=1, source_target_pairs={{4,0},{8,4},{12,8},{16,12},{20,16},{24,20},{28,24},{0,28},{5,1},{9... | collective-permute-start | bytes 12296 | tf_op jit(solution)/shard_map/ppermute | solution.py:34
  32.1 6.4 %collective-permute-start.9 = (f32[1,1,8,128]{3,1,2,0:T(1,128)S(1)}, f32[1,1,8,128]{3,1,2,0:T(1,128)S(1)}, u32[]{:S(2)}, u32[]{:S(2)}) collective-permute-start(f32[1,1,8,128]{3,1,2,0:T(1,128)S(1)} %get-tuple-element.58), channel_id=1, source_target_pairs={{0,4},{4,8},{8,12},{12,16},{16,20},{20,24},{24,28},{28,0},{1,5},{5... | collective-permute-start | bytes 12296 | tf_op jit(solution)/shard_map/ppermute | solution.py:33
  34.1 4.9 %copy-start.5 = (f32[8,8,128]{2,1,0:T(8,128)S(1)}, f32[8,8,128]{2,1,0:T(8,128)}, u32[]{:S(2)}) copy-start(f32[8,8,128]{2,1,0:T(8,128)} %param.41) | copy-start | bytes 98308
  38.5 0.7 copy-start.7
  38.5 1.4 %collective-permute-start.10 = (f32[1,8,1,128]{3,1,2,0:T(8,128)S(1)}, f32[1,8,1,128]{3,1,2,0:T(8,128)S(1)}, u32[]{:S(2)}, u32[]{:S(2)}) collective-permute-start(f32[1,8,1,128]{3,1,2,0:T(8,128)S(1)} %get-tuple-element.55), channel_id=1, source_target_pairs={{1,0},{2,1},{3,2},{0,3},{5,4},{6,5},{7,6},{4,7},{9,8},{10,9},{11,1... | collective-permute-start | bytes 12296 | tf_op jit(solution)/shard_map/ppermute | solution.py:34
  38.6 3.1 %collective-permute-start.11 = (f32[1,8,1,128]{3,1,2,0:T(8,128)S(1)}, f32[1,8,1,128]{3,1,2,0:T(8,128)S(1)}, u32[]{:S(2)}, u32[]{:S(2)}) collective-permute-start(f32[1,8,1,128]{3,1,2,0:T(8,128)S(1)} %get-tuple-element.56), channel_id=1, source_target_pairs={{0,1},{1,2},{2,3},{3,0},{4,5},{5,6},{6,7},{7,4},{8,9},{9,10},{10,1... | collective-permute-start | bytes 12296 | tf_op jit(solution)/shard_map/ppermute | solution.py:33
  41.9 0.7 copy-start.8
  42.8 0.8 copy-start.11
  43.9 3.7 %collective-permute-start.12 = (f32[2,1,8,128]{3,1,2,0:T(1,128)S(1)}, f32[2,1,8,128]{3,1,2,0:T(1,128)S(1)}, u32[]{:S(2)}, u32[]{:S(2)}) collective-permute-start(f32[2,1,8,128]{3,1,2,0:T(1,128)S(1)} %get-tuple-element.33), channel_id=1, source_target_pairs={{4,0},{8,4},{12,8},{16,12},{20,16},{24,20},{28,24},{0,28},{5,1},{9... | collective-permute-start | bytes 24584 | tf_op jit(solution)/shard_map/ppermute | solution.py:34
  44.0 6.4 %collective-permute-start.13 = (f32[2,1,8,128]{3,1,2,0:T(1,128)S(1)}, f32[2,1,8,128]{3,1,2,0:T(1,128)S(1)}, u32[]{:S(2)}, u32[]{:S(2)}) collective-permute-start(f32[2,1,8,128]{3,1,2,0:T(1,128)S(1)} %get-tuple-element.34), channel_id=1, source_target_pairs={{0,4},{4,8},{8,12},{12,16},{16,20},{20,24},{24,28},{28,0},{1,5},{5... | collective-permute-start | bytes 24584 | tf_op jit(solution)/shard_map/ppermute | solution.py:33
  50.5 1.4 %collective-permute-start.14 = (f32[2,8,1,128]{3,1,2,0:T(8,128)S(1)}, f32[2,8,1,128]{3,1,2,0:T(8,128)S(1)}, u32[]{:S(2)}, u32[]{:S(2)}) collective-permute-start(f32[2,8,1,128]{3,1,2,0:T(8,128)S(1)} %get-tuple-element.31), channel_id=1, source_target_pairs={{1,0},{2,1},{3,2},{0,3},{5,4},{6,5},{7,6},{4,7},{9,8},{10,9},{11,1... | collective-permute-start | bytes 24584 | tf_op jit(solution)/shard_map/ppermute | solution.py:34
  50.5 3.2 %collective-permute-start.15 = (f32[2,8,1,128]{3,1,2,0:T(8,128)S(1)}, f32[2,8,1,128]{3,1,2,0:T(8,128)S(1)}, u32[]{:S(2)}, u32[]{:S(2)}) collective-permute-start(f32[2,8,1,128]{3,1,2,0:T(8,128)S(1)} %get-tuple-element.32), channel_id=1, source_target_pairs={{0,1},{1,2},{2,3},{3,0},{4,5},{5,6},{6,7},{7,4},{8,9},{9,10},{10,1... | collective-permute-start | bytes 24584 | tf_op jit(solution)/shard_map/ppermute | solution.py:33
  54.7 0.7 copy-start.4
  55.6 0.9 copy-start.3
  56.7 3.7 %collective-permute-start.16 = (f32[1,1,8,128]{3,1,2,0:T(1,128)S(1)}, f32[1,1,8,128]{3,1,2,0:T(1,128)S(1)}, u32[]{:S(2)}, u32[]{:S(2)}) collective-permute-start(f32[1,1,8,128]{3,1,2,0:T(1,128)S(1)} %get-tuple-element.49), channel_id=1, source_target_pairs={{4,0},{8,4},{12,8},{16,12},{20,16},{24,20},{28,24},{0,28},{5,1},{9... | collective-permute-start | bytes 12296 | tf_op jit(solution)/shard_map/ppermute | solution.py:34
  56.8 6.4 %collective-permute-start.17 = (f32[1,1,8,128]{3,1,2,0:T(1,128)S(1)}, f32[1,1,8,128]{3,1,2,0:T(1,128)S(1)}, u32[]{:S(2)}, u32[]{:S(2)}) collective-permute-start(f32[1,1,8,128]{3,1,2,0:T(1,128)S(1)} %get-tuple-element.50), channel_id=1, source_target_pairs={{0,4},{4,8},{8,12},{12,16},{16,20},{20,24},{24,28},{28,0},{1,5},{5... | collective-permute-start | bytes 12296 | tf_op jit(solution)/shard_map/ppermute | solution.py:33
  63.2 1.4 %collective-permute-start.18 = (f32[1,8,1,128]{3,1,2,0:T(8,128)S(1)}, f32[1,8,1,128]{3,1,2,0:T(8,128)S(1)}, u32[]{:S(2)}, u32[]{:S(2)}) collective-permute-start(f32[1,8,1,128]{3,1,2,0:T(8,128)S(1)} %get-tuple-element.47), channel_id=1, source_target_pairs={{1,0},{2,1},{3,2},{0,3},{5,4},{6,5},{7,6},{4,7},{9,8},{10,9},{11,1... | collective-permute-start | bytes 12296 | tf_op jit(solution)/shard_map/ppermute | solution.py:34
  63.3 3.1 %collective-permute-start.19 = (f32[1,8,1,128]{3,1,2,0:T(8,128)S(1)}, f32[1,8,1,128]{3,1,2,0:T(8,128)S(1)}, u32[]{:S(2)}, u32[]{:S(2)}) collective-permute-start(f32[1,8,1,128]{3,1,2,0:T(8,128)S(1)} %get-tuple-element.48), channel_id=1, source_target_pairs={{0,1},{1,2},{2,3},{3,0},{4,5},{5,6},{6,7},{7,4},{8,9},{9,10},{10,1... | collective-permute-start | bytes 12296 | tf_op jit(solution)/shard_map/ppermute | solution.py:33
  94.0 3.7 %collective-permute-start.20 = (f32[1,1,8,128]{3,1,2,0:T(1,128)S(1)}, f32[1,1,8,128]{3,1,2,0:T(1,128)S(1)}, u32[]{:S(2)}, u32[]{:S(2)}) collective-permute-start(f32[1,1,8,128]{3,1,2,0:T(1,128)S(1)} %get-tuple-element.41), channel_id=1, source_target_pairs={{4,0},{8,4},{12,8},{16,12},{20,16},{24,20},{28,24},{0,28},{5,1},{9... | collective-permute-start | bytes 12296 | tf_op jit(solution)/shard_map/ppermute | solution.py:34
  96.1 6.3 %collective-permute-start.21 = (f32[1,1,8,128]{3,1,2,0:T(1,128)S(1)}, f32[1,1,8,128]{3,1,2,0:T(1,128)S(1)}, u32[]{:S(2)}, u32[]{:S(2)}) collective-permute-start(f32[1,1,8,128]{3,1,2,0:T(1,128)S(1)} %get-tuple-element.42), channel_id=1, source_target_pairs={{0,4},{4,8},{8,12},{12,16},{16,20},{20,24},{24,28},{28,0},{1,5},{5... | collective-permute-start | bytes 12296 | tf_op jit(solution)/shard_map/ppermute | solution.py:33
  102.4 1.4 %collective-permute-start.22 = (f32[1,8,1,128]{3,1,2,0:T(8,128)S(1)}, f32[1,8,1,128]{3,1,2,0:T(8,128)S(1)}, u32[]{:S(2)}, u32[]{:S(2)}) collective-permute-start(f32[1,8,1,128]{3,1,2,0:T(8,128)S(1)} %get-tuple-element.39), channel_id=1, source_target_pairs={{1,0},{2,1},{3,2},{0,3},{5,4},{6,5},{7,6},{4,7},{9,8},{10,9},{11,1... | collective-permute-start | bytes 12296 | tf_op jit(solution)/shard_map/ppermute | solution.py:34
  102.5 3.1 %collective-permute-start.23 = (f32[1,8,1,128]{3,1,2,0:T(8,128)S(1)}, f32[1,8,1,128]{3,1,2,0:T(8,128)S(1)}, u32[]{:S(2)}, u32[]{:S(2)}) collective-permute-start(f32[1,8,1,128]{3,1,2,0:T(8,128)S(1)} %get-tuple-element.40), channel_id=1, source_target_pairs={{0,1},{1,2},{2,3},{3,0},{4,5},{5,6},{6,7},{7,4},{8,9},{9,10},{10,1... | collective-permute-start | bytes 12296 | tf_op jit(solution)/shard_map/ppermute | solution.py:33
